TPU v7x, 32 devices: a whole 2x2x4 slice. The times are simulated.
32 devices in a mesh: samples: 4 (over y, x), features: 4 (over z), rhs: 2 (over core).
Axes of the slice: x: 2, y: 2, z: 4, core: 2. Of those that a mesh axis runs over, the one named last changes fastest.
Arguments:
- design: bfloat16 [32768, 32768], P(('samples', 'rhs'), 'features'), may hold values from -0.03125 to 0.03125
- right_side: float32 [32768, 64], P('features', 'rhs'), may hold values from -6 to 6
- factor: bfloat16 [32768, 768], P('features', 'rhs'), may hold values from -0.03125 to 0.03125
- nystrom_values: float32 [768], replicated, may hold values from 0.5 to 3
Outputs:
- solution: float32 [32768, 64], P('features', 'rhs')
- residual: float32 [32768, 64], P('features', 'rhs')
All inputs are finite; a program needn't handle non-finite values.
Results may differ from a plain program's by a relative error of at most 0.0181.
Values may be sent and summed in bfloat16 or wider, within the bound.
A program may use at most 192 MiB of HBM per device.

v0:
```python
import jax
import jax.numpy as jnp
from jax import lax
from jax.sharding import PartitionSpec as P

ITERS = 3
ridge_weight = 1.0


def inner_prod(left, right):
    return lax.dot_general(
        left,
        right,
        (((0,), (0,)), ((), ())),
        precision=lax.Precision.HIGHEST,
        preferred_element_type=jnp.float32,
    )


def split_parts(values):
    upper = values.astype(jnp.bfloat16)
    widened = lax.optimization_barrier(upper).astype(jnp.float32)
    lower = (values - widened).astype(jnp.bfloat16)
    return (upper, lower)


def factor_inner(factor_narrow, values):
    upper, lower = split_parts(values)
    dims = (((0,), (0,)), ((), ()))
    first = lax.dot_general(factor_narrow, upper, dims, preferred_element_type=jnp.float32)
    second = lax.dot_general(factor_narrow, lower, dims, preferred_element_type=jnp.float32)
    return first + second


def factor_times(factor_narrow, values):
    upper, lower = split_parts(values)
    first = jnp.dot(factor_narrow, upper, preferred_element_type=jnp.float32)
    second = jnp.dot(factor_narrow, lower, preferred_element_type=jnp.float32)
    return first + second


def shards(design, right_side, factor, nystrom_values):
    feat_rows, col_share = right_side.shape
    shrink = (1.0 + jnp.min(nystrom_values)) / (1.0 + nystrom_values) - 1.0
    columns = lax.all_gather(right_side, "rhs", axis=1, tiled=True)
    residual = columns
    basis_rows = lax.all_gather(factor, "rhs", axis=1, tiled=True)

    def totals(values):
        return lax.psum(values, "features")

    def expand(projected):
        return factor_times(basis_rows, shrink[:, None] * projected)

    projected = totals(factor_inner(basis_rows, residual))
    direction = residual + expand(projected)
    solution = jnp.zeros_like(residual)
    for iteration in range(ITERS):
        narrow = direction.astype(jnp.bfloat16)
        apply_partial_value = jnp.dot(design, narrow, preferred_element_type=jnp.float32)
        narrow_images = lax.psum(apply_partial_value, "features").astype(jnp.bfloat16)
        feature_term = lax.dot_general(
            design, narrow_images, (((0,), (0,)), ((), ())), preferred_element_type=jnp.float32
        )
        summed = lax.psum(feature_term, ("samples", "rhs"))
        applied = summed + ridge_weight * direction
        gram_block, cross_term, image_res, image_image, factor_image = totals(
            (
                inner_prod(direction, applied),
                inner_prod(direction, residual),
                inner_prod(applied, residual),
                inner_prod(applied, applied),
                factor_inner(basis_rows, applied),
            )
        )
        gram_block = 0.5 * (gram_block + gram_block.T)
        chol_lower = jnp.linalg.cholesky(gram_block)
        unit_dir = jax.scipy.linalg.solve_triangular(chol_lower, direction.T, lower=True).T
        unit_img = jax.scipy.linalg.solve_triangular(chol_lower, applied.T, lower=True).T
        step_coef = jax.scipy.linalg.solve_triangular(chol_lower, cross_term, lower=True)
        solution = solution + jnp.dot(unit_dir, step_coef, precision=lax.Precision.HIGHEST)
        residual = residual - jnp.dot(unit_img, step_coef, precision=lax.Precision.HIGHEST)
        if iteration + 1 < ITERS:
            back_step = jax.scipy.linalg.solve_triangular(
                chol_lower, step_coef, lower=True, trans=1
            )
            projected = projected - jnp.dot(
                factor_image, back_step, precision=lax.Precision.HIGHEST
            )
            scaled = residual + expand(projected)
            image_new = image_res - jnp.dot(image_image, back_step, precision=lax.Precision.HIGHEST)
            image_new = image_new + inner_prod(factor_image, shrink[:, None] * projected)
            next_coef = -jax.scipy.linalg.solve_triangular(chol_lower, image_new, lower=True)
            direction = scaled + jnp.dot(unit_dir, next_coef, precision=lax.Precision.HIGHEST)
    column_start = lax.axis_index("rhs") * col_share
    out_sol = lax.dynamic_slice_in_dim(solution, column_start, col_share, 1)
    out_res = lax.dynamic_slice_in_dim(residual, column_start, col_share, 1)
    return (out_sol, out_res)


def solution(mesh):
    placed = (P(("samples", "rhs"), "features"), P("features", "rhs"), P("features", "rhs"), P())
    return jax.shard_map(
        shards,
        mesh=mesh,
        in_specs=placed,
        out_specs=(P("features", "rhs"), P("features", "rhs")),
        check_vma=False,
    )
```

profile of v0, /device:TPU:0, one launch (start us, length us, event | category | flops | bytes accessed | tf_op | source)
XLA Modules:
  0.0 853.2 jit_solution(9998928612973178029)
XLA Ops:
  10.0 12.9 %all-gather.3.cloned.1.call-done = f32[8192,64]{0,1:T(8,128)} async-done(((f32[8192,32]{0,1:T(8,128)}), f32[8192,64]{0,1:T(8,128)}) %all-gather.3.cloned.1.call-update) | async-done | bytes 2097168 | tf_op jit(solution)/shard_map/all_gather | solution.py:45
  24.7 25.6 %all-gather.5.cloned.1.call-done = bf16[8192,768]{1,0:T(8,128)(2,1)} async-done(((bf16[8192,384]{1,0:T(8,128)(2,1)}), bf16[8192,768]{1,0:T(8,128)(2,1)}) %all-gather.5.cloned.1.call-update) | async-done | bytes 12582928 | tf_op jit(solution)/shard_map/all_gather | solution.py:47
  50.3 7.0 convolution_bitcast_fusion.6
  61.5 36.2 %all-reduce.15.cloned.1.call-done = f32[768,64]{0,1:T(8,128)} async-done(((f32[768,64]{0,1:T(8,128)}), f32[768,64]{0,1:T(8,128)}) %all-reduce.15.cloned.1.call-update) | async-done | bytes 196624 | tf_op jit(solution)/shard_map/psum | solution.py:50
  98.7 8.5 fusion.67
  107.2 9.8 %fusion.3 = f32[8192,64]{0,1:T(8,128)} fusion(f32[8192,64]{0,1:T(8,128)S(1)} %copy-done.1, f32[64,8192]{1,0:T(8,128)S(1)} %fusion.67, bf16[8192,768]{1,0:T(8,128)(2,1)} %all-gather.5.cloned.1.call-done, bf16[768,64]{0,1:T(8,128)(2,1)S(1)} %multiply_convert_fusion, f32[768,64]{0,1:T(8,128)S(1)} %copy-done.19, f32[768]{0:T(1024)S(1)} %divide_add_fusion), kind=kOutput, calls=%fused_computation.13 | convolution fusion | flops 806551552 | bytes 19172352 | tf_op jit(solution)/shard_map/dot_general | solution.py:38
  117.1 30.4 %convolution_bitcast_fusion.5 = f32[4096,64]{0,1:T(8,128)S(1)} fusion(bf16[4096,8192]{1,0:T(8,128)(2,1)} %param.11, f32[8192,64]{0,1:T(8,128)} %fusion.3), kind=kOutput, calls=%fused_computation.18 | convolution fusion | flops 4295491584 | bytes 70254592 | tf_op jit(solution)/shard_map/dot_general | solution.py:60
  147.4 42.8 %all-reduce.30 = bf16[4096,64]{0,1:T(8,128)(2,1)} all-reduce(f32[4096,64]{0,1:T(8,128)S(1)} %convolution_bitcast_fusion.5), channel_id=1, replica_groups=mesh['samples'=4,'features'=4,'rhs'=2] {'features'}, use_global_device_ids=true, to_apply=%region_2.0 | all-reduce | flops 262144 | bytes 1572864 | tf_op jit(solution)/shard_map/psum | solution.py:61
  190.2 25.9 %convolution_bitcast_fusion.2 = f32[8192,64]{0,1:T(8,128)} fusion(bf16[4096,8192]{1,0:T(8,128)(2,1)} %param.11, bf16[4096,64]{0,1:T(8,128)(2,1)} %all-reduce.30), kind=kOutput, calls=%fused_computation.10 | convolution fusion | flops 4294967296 | bytes 69730304 | tf_op jit(solution)/shard_map/dot_general | solution.py:62
  220.2 57.3 %all-reduce.17.cloned.1.call-done = f32[8192,64]{0,1:T(8,128)} async-done(((f32[8192,64]{0,1:T(8,128)}), f32[8192,64]{0,1:T(8,128)}) %all-reduce.17.cloned.1.call-update) | async-done | bytes 2097168 | tf_op jit(solution)/shard_map/psum | solution.py:65
  287.3 6.8 fusion.71
  294.2 7.6 fusion.22
  302.0 19.4 %all-reduce.29.cloned.1.call-done = (f32[64,64]{1,0:T(8,128)}, f32[64,64]{1,0:T(8,128)}, f32[64,64]{1,0:T(8,128)}, f32[64,64]{1,0:T(8,128)}) async-done(((f32[64,64]{1,0:T(8,128)}, f32[64,64]{1,0:T(8,128)}, f32[64,64]{1,0:T(8,128)}, f32[64,64]{1,0:T(8,128)}), (f32[64,64]{1,0:T(8,128)}, f32[64,64]{1,0:T(8,128)}, f32[64,64]{1,0:T(8,128)}, f32[64,64]{1,0:T(8,128)})) %all-reduce.29.cloned.1.call-update) | async-done | bytes 65552 | tf_op jit(solution)/shard_map/psum | solution.py:50
  344.5 14.6 %all-reduce.19.cloned.1.call-done = f32[768,64]{0,1:T(8,128)} async-done(((f32[768,64]{0,1:T(8,128)}), f32[768,64]{0,1:T(8,128)}) %all-reduce.19.cloned.1.call-update) | async-done | bytes 196624 | tf_op jit(solution)/shard_map/psum | solution.py:50
  362.1 8.4 fusion.72
  370.6 8.6 %fusion.4 = f32[8192,64]{0,1:T(8,128)S(1)} fusion(f32[8192,64]{0,1:T(8,128)S(1)} %convolution_subtract_fusion.1, f32[64,8192]{1,0:T(8,128)S(1)} %fusion.72, bf16[8192,768]{1,0:T(8,128)(2,1)} %all-gather.5.cloned.1.call-done, bf16[768,64]{0,1:T(8,128)(2,1)S(1)} %get-tuple-element.20, f32[768,64]{0,1:T(8,128)S(1)} %get-tuple-element.21, ...), kind=kOutput, calls=%fused_computation.14 | convolution fusion | flops 806551552 | bytes 19172352 | tf_op jit(solution)/shard_map/dot_general | solution.py:38
  381.5 27.8 %convolution_bitcast_fusion.4 = f32[4096,64]{0,1:T(8,128)S(1)} fusion(bf16[4096,8192]{1,0:T(8,128)(2,1)} %param.11, f32[8192,64]{0,1:T(8,128)S(1)} %convolution_add_fusion.2), kind=kOutput, calls=%fused_computation.17 | convolution fusion | flops 4295491584 | bytes 70254592 | tf_op jit(solution)/shard_map/dot_general | solution.py:60
  409.4 42.1 %all-reduce.31 = bf16[4096,64]{0,1:T(8,128)(2,1)} all-reduce(f32[4096,64]{0,1:T(8,128)S(1)} %convolution_bitcast_fusion.4), channel_id=1, replica_groups=mesh['samples'=4,'features'=4,'rhs'=2] {'features'}, use_global_device_ids=true, to_apply=%region_11.0 | all-reduce | flops 262144 | bytes 1572864 | tf_op jit(solution)/shard_map/psum | solution.py:61
  451.5 25.9 %convolution_bitcast_fusion.1 = f32[8192,64]{0,1:T(8,128)} fusion(bf16[4096,8192]{1,0:T(8,128)(2,1)} %param.11, bf16[4096,64]{0,1:T(8,128)(2,1)} %all-reduce.31), kind=kOutput, calls=%fused_computation.5 | convolution fusion | flops 4294967296 | bytes 69730304 | tf_op jit(solution)/shard_map/dot_general | solution.py:62
  481.9 57.4 %all-reduce.21.cloned.1.call-done = f32[8192,64]{0,1:T(8,128)} async-done(((f32[8192,64]{0,1:T(8,128)}), f32[8192,64]{0,1:T(8,128)}) %all-reduce.21.cloned.1.call-update) | async-done | bytes 2097168 | tf_op jit(solution)/shard_map/psum | solution.py:65
  549.5 6.8 fusion.78
  556.4 7.6 fusion.23
  564.2 19.4 %all-reduce.27.cloned.1.call-done = (f32[64,64]{1,0:T(8,128)}, f32[64,64]{1,0:T(8,128)}, f32[64,64]{1,0:T(8,128)}, f32[64,64]{1,0:T(8,128)}) async-done(((f32[64,64]{1,0:T(8,128)}, f32[64,64]{1,0:T(8,128)}, f32[64,64]{1,0:T(8,128)}, f32[64,64]{1,0:T(8,128)}), (f32[64,64]{1,0:T(8,128)}, f32[64,64]{1,0:T(8,128)}, f32[64,64]{1,0:T(8,128)}, f32[64,64]{1,0:T(8,128)})) %all-reduce.27.cloned.1.call-update) | async-done | bytes 65552 | tf_op jit(solution)/shard_map/psum | solution.py:50
  585.3 5.8 cholesky.70
  606.6 14.8 %all-reduce.23.cloned.1.call-done = f32[768,64]{0,1:T(8,128)} async-done(((f32[768,64]{0,1:T(8,128)}), f32[768,64]{0,1:T(8,128)}) %all-reduce.23.cloned.1.call-update) | async-done | bytes 196624 | tf_op jit(solution)/shard_map/psum | solution.py:50
  624.5 8.4 fusion.79
  632.9 8.6 %fusion.5 = f32[8192,64]{0,1:T(8,128)S(1)} fusion(f32[8192,64]{0,1:T(8,128)S(1)} %convolution_subtract_fusion, f32[64,8192]{1,0:T(8,128)S(1)} %fusion.79, bf16[8192,768]{1,0:T(8,128)(2,1)} %all-gather.5.cloned.1.call-done, f32[768,64]{0,1:T(8,128)S(1)} %get-tuple-element.23, bf16[768,64]{0,1:T(8,128)(2,1)S(1)} %get-tuple-element.22), kind=kOutput, calls=%fused_computation.15 | convolution fusion | flops 806502400 | bytes 19169280 | tf_op jit(solution)/shard_map/dot_general | solution.py:38
  644.0 27.1 %convolution_bitcast_fusion.3 = f32[4096,64]{0,1:T(8,128)S(1)} fusion(bf16[4096,8192]{1,0:T(8,128)(2,1)} %param.11, f32[8192,64]{0,1:T(8,128)S(1)} %convolution_add_fusion), kind=kOutput, calls=%fused_computation.16 | convolution fusion | flops 4295491584 | bytes 70254592 | tf_op jit(solution)/shard_map/dot_general | solution.py:60
  671.1 42.1 %all-reduce.32 = bf16[4096,64]{0,1:T(8,128)(2,1)} all-reduce(f32[4096,64]{0,1:T(8,128)S(1)} %convolution_bitcast_fusion.3), channel_id=1, replica_groups=mesh['samples'=4,'features'=4,'rhs'=2] {'features'}, use_global_device_ids=true, to_apply=%region_18.0 | all-reduce | flops 262144 | bytes 1572864 | tf_op jit(solution)/shard_map/psum | solution.py:61
  713.2 25.9 %convolution_bitcast_fusion = f32[8192,64]{0,1:T(8,128)} fusion(bf16[4096,8192]{1,0:T(8,128)(2,1)} %param.11, bf16[4096,64]{0,1:T(8,128)(2,1)} %all-reduce.32), kind=kOutput, calls=%fused_computation | convolution fusion | flops 4294967296 | bytes 69730304 | tf_op jit(solution)/shard_map/dot_general | solution.py:62
  750.0 50.6 %all-reduce.25.cloned.1.call-done = f32[8192,64]{0,1:T(8,128)} async-done(((f32[8192,64]{0,1:T(8,128)}), f32[8192,64]{0,1:T(8,128)}) %all-reduce.25.cloned.1.call-update) | async-done | bytes 2097168 | tf_op jit(solution)/shard_map/psum | solution.py:65
  804.1 19.8 %all-reduce = (f32[64,64]{1,0:T(8,128)S(1)}, f32[64,64]{1,0:T(8,128)S(1)}) all-reduce(f32[64,64]{1,0:T(8,128)S(1)} %fusion.19, f32[64,64]{1,0:T(8,128)S(1)} %fusion.83), channel_id=1, replica_groups=mesh['samples'=4,'features'=4,'rhs'=2] {'features'}, use_global_device_ids=true, to_apply=%region_20.25 | all-reduce | flops 8192 | bytes 65536 | tf_op jit(solution)/shard_map/psum | solution.py:50
  (149 shorter events, 125.3 us)
Async XLA Ops:
  7.2 15.7 %all-gather.3.cloned.1.call-start = ((), (), s32[]{:S(2)}) async-start(), calls=%async_computation | async-start | bytes 3145728 | tf_op jit(solution)/shard_map/all_gather | solution.py:45
  7.9 42.4 %all-gather.5.cloned.1.call-start = ((), (), s32[]{:S(2)}) async-start(), calls=%async_computation.1 | async-start | bytes 18874368 | tf_op jit(solution)/shard_map/all_gather | solution.py:47
  8.7 89.1 %all-reduce.15.cloned.1.call-start = ((), (), s32[]{:S(2)}) async-start(), calls=%async_computation.2 | async-start | bytes 393216 | tf_op jit(solution)/shard_map/psum | solution.py:50
  22.8 27.4 %copy-start.1 = (f32[8192,64]{0,1:T(8,128)S(1)}, f32[8192,64]{0,1:T(8,128)}, u32[]{:S(2)}) copy-start(f32[8192,64]{0,1:T(8,128)} %all-gather.3.cloned.1.call-done) | copy-start | bytes 6291460
  50.3 8.2 copy-start
  61.5 216.0 %all-reduce.17.cloned.1.call-start = ((), (), s32[]{:S(2)}) async-start(), calls=%async_computation.3 | async-start | bytes 4194304 | tf_op jit(solution)/shard_map/psum | solution.py:65
  98.7 8.5 copy-start.19
  216.2 105.3 %all-reduce.29.cloned.1.call-start = ((), (), s32[]{:S(2)}) async-start(), calls=%async_computation.9 | async-start | bytes 262144 | tf_op jit(solution)/shard_map/psum | solution.py:50
  280.0 2.4 copy-start.4
  282.4 2.4 copy-start.2
  287.3 71.8 %all-reduce.19.cloned.1.call-start = ((), (), s32[]{:S(2)}) async-start(), calls=%async_computation.4 | async-start | bytes 393216 | tf_op jit(solution)/shard_map/psum | solution.py:50
  301.8 237.5 %all-reduce.21.cloned.1.call-start = ((), (), s32[]{:S(2)}) async-start(), calls=%async_computation.5 | async-start | bytes 4194304 | tf_op jit(solution)/shard_map/psum | solution.py:65
  340.0 2.2 copy-start.3
  342.2 19.4 %copy-start.24 = (f32[64,64]{1,0:T(8,128)S(1)}, f32[64,64]{1,0:T(8,128)}, u32[]{:S(2)}) copy-start(f32[64,64]{1,0:T(8,128)} %get-tuple-element.14) | copy-start | bytes 49156
  342.2 19.4 %copy-start.25 = (f32[64,64]{1,0:T(8,128)S(1)}, f32[64,64]{1,0:T(8,128)}, u32[]{:S(2)}) copy-start(f32[64,64]{1,0:T(8,128)} %get-tuple-element.15) | copy-start | bytes 49156
  344.3 26.2 %copy-start.7 = (f32[8192,64]{0,1:T(8,128)}, f32[8192,64]{0,1:T(8,128)S(1)}, u32[]{:S(2)}) copy-start(f32[8192,64]{0,1:T(8,128)S(1)} %convolution_subtract_fusion.1) | copy-start | bytes 6291460
  370.5 8.7 %copy-start.13 = (f32[64,8192]{1,0:T(8,128)S(1)}, f32[64,8192]{1,0:T(8,128)}, u32[]{:S(2)}) copy-start(f32[64,8192]{1,0:T(8,128)} %fusion.16) | copy-start | bytes 6291460
  381.5 96.4 %copy-start.5 = (f32[8192,64]{0,1:T(8,128)}, f32[8192,64]{0,1:T(8,128)S(1)}, u32[]{:S(2)}) copy-start(f32[8192,64]{0,1:T(8,128)S(1)} %convolution_add_fusion.2) | copy-start | bytes 6291460
  477.5 106.1 %all-reduce.27.cloned.1.call-start = ((), (), s32[]{:S(2)}) async-start(), calls=%async_computation.8 | async-start | bytes 262144 | tf_op jit(solution)/shard_map/psum | solution.py:50
  539.3 2.9 copy-start.8
  544.6 2.4 copy-start.6
  549.5 72.0 %all-reduce.23.cloned.1.call-start = ((), (), s32[]{:S(2)}) async-start(), calls=%async_computation.6 | async-start | bytes 393216 | tf_op jit(solution)/shard_map/psum | solution.py:50
  564.0 236.7 %all-reduce.25.cloned.1.call-start = ((), (), s32[]{:S(2)}) async-start(), calls=%async_computation.7 | async-start | bytes 4194304 | tf_op jit(solution)/shard_map/psum | solution.py:65
  602.2 2.2 copy-start.9
  604.4 19.7 %copy-start.22 = (f32[64,64]{1,0:T(8,128)S(1)}, f32[64,64]{1,0:T(8,128)}, u32[]{:S(2)}) copy-start(f32[64,64]{1,0:T(8,128)} %get-tuple-element.10) | copy-start | bytes 49156
  604.4 19.7 %copy-start.23 = (f32[64,64]{1,0:T(8,128)S(1)}, f32[64,64]{1,0:T(8,128)}, u32[]{:S(2)}) copy-start(f32[64,64]{1,0:T(8,128)} %get-tuple-element.11) | copy-start | bytes 49156
  606.5 26.5 %copy-start.10 = (f32[8192,64]{0,1:T(8,128)}, f32[8192,64]{0,1:T(8,128)S(1)}, u32[]{:S(2)}) copy-start(f32[8192,64]{0,1:T(8,128)S(1)} %convolution_subtract_fusion) | copy-start | bytes 6291460
  632.9 8.6 %copy-start.14 = (f32[64,8192]{1,0:T(8,128)S(1)}, f32[64,8192]{1,0:T(8,128)}, u32[]{:S(2)}) copy-start(f32[64,8192]{1,0:T(8,128)} %fusion.12) | copy-start | bytes 6291460
  739.9 5.0 copy-start.15
  744.9 3.3 copy-start.11
  840.4 4.1 copy-start.18
  842.4 2.2 copy-start.17
  (7 other events, 11.6 us)
Sparse Core Ops, SparseCore 0:
  9.5 13.2 all-gather.2
  24.4 25.8 all-gather.4
  61.6 36.1 all-reduce.14
  216.3 61.1 all-reduce.16
  287.4 33.9 all-reduce.28
  324.2 34.8 all-reduce.18
  477.6 61.6 all-reduce.20
  549.6 33.9 all-reduce.26
  586.5 34.9 all-reduce.22
  739.3 61.3 all-reduce.24
where the time goes:
time: 862 us; the launch traced here: 853 us
  matrix products  328 us (38%)
  waiting for transfers between devices  310 us (36%)
  blocking collectives  147 us (17%)
  other arithmetic  47.9 us (6%)
  between operations  15.6 us (2%)
    psum x3, waiting for transfers between devices, shards(): summed = lax.psum(feature_term, ('samples', 'rhs'))  165 us
    psum x3, blocking collectives, shards(): lax.psum(apply_partial_value, 'features').astype(jnp.bfloat16)  127 us
    psum x5, waiting for transfers between devices, totals(): return lax.psum(values, 'features')  105 us
    dot_general x3, matrix products, shards(): jnp.dot(design, narrow, preferred_element_type=jnp.float32)  85.3 us
    dot_general x3, matrix products, shards(): lax.dot_general(design, narrow_images, (((0,), (0,)), ((), ())), preferre...  77.8 us
    dot_general x12, matrix products, inner_prod(): lax.dot_general(left, right, (((0,), (0,)), ((), ())), precision=lax.Prec...  30.3 us
    dot_general x3, matrix products, factor_times(): second = jnp.dot(factor_narrow, lower, preferred_element_type=jnp.float32)  27.1 us
    all_gather x1, waiting for transfers between devices, shards(): basis_rows = lax.all_gather(factor, 'rhs', axis=1, tiled=True)  25.6 us
  transfers between devices with their start and end apart: 10, of which 10 were waited for; matrix products, arithmetic and copies ran while one was open for 11% of the time, Pallas kernels for 0%

commit v1 on v0

--- a/solution.py
+++ b/solution.py
@@ -1,10 +1,21 @@
+import functools
 import jax
 import jax.numpy as jnp
 from jax import lax
 from jax.sharding import PartitionSpec as P
+from jax.lax import psum
 
 ITERS = 3
 ridge_weight = 1.0
+
+
+def begin_boxes_on_mesh(block_in, axis_name, lane_axis):
+    for q in (axis_name, lane_axis):
+        block_in = psum(block_in, q)
+    return block_in
+
+
+_obtain_indices = functools.partial(begin_boxes_on_mesh, axis_name="rhs", lane_axis="samples")
 
 
 def inner_prod(left, right):
@@ -62,7 +73,7 @@
         feature_term = lax.dot_general(
             design, narrow_images, (((0,), (0,)), ((), ())), preferred_element_type=jnp.float32
         )
-        summed = lax.psum(feature_term, ("samples", "rhs"))
+        summed = _obtain_indices(feature_term)
         applied = summed + ridge_weight * direction
         gram_block, cross_term, image_res, image_image, factor_image = totals(
             (

time: 862 us -> 963 us (1.12)
  waiting for transfers between devices: 310 us -> 411 us
    psum x3 -> x6, waiting for transfers between devices: 165 us -> 265 us  [begin_boxes_on_mesh(): block_in = psum(block_in, q)]
  transfers between devices with their start and end apart: 10 -> 13, of which waited for: 10 -> 13; matrix products, arithmetic and copies ran while one was open for 11% -> 10% of each run, Pallas kernels for 0% -> 0%
where the time goes in v1:
time: 963 us; the launch traced here: 954 us
  waiting for transfers between devices  411 us (43%)
  matrix products  328 us (34%)
  blocking collectives  147 us (15%)
  other arithmetic  47.9 us (5%)
  between operations  15.4 us (2%)
    psum x6, waiting for transfers between devices, begin_boxes_on_mesh(): block_in = psum(block_in, q)  265 us
    psum x3, blocking collectives, shards(): lax.psum(apply_partial_value, 'features').astype(jnp.bfloat16)  127 us
    psum x5, waiting for transfers between devices, totals(): return lax.psum(values, 'features')  107 us
    dot_general x3, matrix products, shards(): jnp.dot(design, narrow, preferred_element_type=jnp.float32)  85.3 us
    dot_general x3, matrix products, shards(): lax.dot_general(design, narrow_images, (((0,), (0,)), ((), ())), preferre...  77.8 us
    dot_general x12, matrix products, inner_prod(): lax.dot_general(left, right, (((0,), (0,)), ((), ())), precision=lax.Prec...  30.3 us
    dot_general x3, matrix products, factor_times(): second = jnp.dot(factor_narrow, lower, preferred_element_type=jnp.float32)  27.1 us
    all_gather x1, waiting for transfers between devices, shards(): basis_rows = lax.all_gather(factor, 'rhs', axis=1, tiled=True)  25.6 us
  transfers between devices with their start and end apart: 13, of which 13 were waited for; matrix products, arithmetic and copies ran while one was open for 10% of the time, Pallas kernels for 0%

profile of v1, /device:TPU:0, one launch (start us, length us, event | category | flops | bytes accessed | tf_op | source)
XLA Modules:
  0.0 954.5 jit_solution(14918473197212958825)
XLA Ops:
  10.0 12.9 %all-gather.3.cloned.1.call-done = f32[8192,64]{0,1:T(8,128)} async-done(((f32[8192,32]{0,1:T(8,128)}), f32[8192,64]{0,1:T(8,128)}) %all-gather.3.cloned.1.call-update) | async-done | bytes 2097168 | tf_op jit(solution)/shard_map/all_gather | solution.py:56
  24.7 25.6 %all-gather.5.cloned.1.call-done = bf16[8192,768]{1,0:T(8,128)(2,1)} async-done(((bf16[8192,384]{1,0:T(8,128)(2,1)}), bf16[8192,768]{1,0:T(8,128)(2,1)}) %all-gather.5.cloned.1.call-update) | async-done | bytes 12582928 | tf_op jit(solution)/shard_map/all_gather | solution.py:58
  50.3 7.0 convolution_bitcast_fusion.6
  61.5 36.2 %all-reduce.18.cloned.1.call-done = f32[768,64]{0,1:T(8,128)} async-done(((f32[768,64]{0,1:T(8,128)}), f32[768,64]{0,1:T(8,128)}) %all-reduce.18.cloned.1.call-update) | async-done | bytes 196624 | tf_op jit(solution)/shard_map/psum | solution.py:61
  98.7 8.5 fusion.67
  107.2 9.8 %fusion.3 = f32[8192,64]{0,1:T(8,128)} fusion(f32[8192,64]{0,1:T(8,128)S(1)} %copy-done.1, f32[64,8192]{1,0:T(8,128)S(1)} %fusion.67, bf16[8192,768]{1,0:T(8,128)(2,1)} %all-gather.5.cloned.1.call-done, bf16[768,64]{0,1:T(8,128)(2,1)S(1)} %multiply_convert_fusion, f32[768,64]{0,1:T(8,128)S(1)} %copy-done.19, f32[768]{0:T(1024)S(1)} %divide_add_fusion), kind=kOutput, calls=%fused_computation.13 | convolution fusion | flops 806551552 | bytes 19172352 | tf_op jit(solution)/shard_map/dot_general | solution.py:49
  117.1 30.4 %convolution_bitcast_fusion.5 = f32[4096,64]{0,1:T(8,128)S(1)} fusion(bf16[4096,8192]{1,0:T(8,128)(2,1)} %param.11, f32[8192,64]{0,1:T(8,128)} %fusion.3), kind=kOutput, calls=%fused_computation.18 | convolution fusion | flops 4295491584 | bytes 70254592 | tf_op jit(solution)/shard_map/dot_general | solution.py:71
  147.4 42.8 %all-reduce.39 = bf16[4096,64]{0,1:T(8,128)(2,1)} all-reduce(f32[4096,64]{0,1:T(8,128)S(1)} %convolution_bitcast_fusion.5), channel_id=1, replica_groups=mesh['samples'=4,'features'=4,'rhs'=2] {'features'}, use_global_device_ids=true, to_apply=%region_2.0 | all-reduce | flops 262144 | bytes 1572864 | tf_op jit(solution)/shard_map/psum | solution.py:72
  190.2 25.9 %convolution_bitcast_fusion.2 = f32[8192,64]{0,1:T(8,128)} fusion(bf16[4096,8192]{1,0:T(8,128)(2,1)} %param.11, bf16[4096,64]{0,1:T(8,128)(2,1)} %all-reduce.39), kind=kOutput, calls=%fused_computation.10 | convolution fusion | flops 4294967296 | bytes 69730304 | tf_op jit(solution)/shard_map/dot_general | solution.py:73
  216.2 20.8 %all-reduce.20.cloned.1.call-done = f32[8192,64]{0,1:T(8,128)} async-done(((f32[8192,64]{0,1:T(8,128)}), f32[8192,64]{0,1:T(8,128)}) %all-reduce.20.cloned.1.call-update) | async-done | bytes 2097168 | tf_op jit(solution)/shard_map/psum | solution.py:14
  241.1 69.6 %all-reduce.22.cloned.1.call-done = f32[8192,64]{0,1:T(8,128)} async-done(((f32[8192,64]{0,1:T(8,128)}), f32[8192,64]{0,1:T(8,128)}) %all-reduce.22.cloned.1.call-update) | async-done | bytes 2097168 | tf_op jit(solution)/shard_map/psum | solution.py:14
  327.3 7.6 fusion.22
  335.2 20.4 %all-reduce.38.cloned.1.call-done = (f32[64,64]{1,0:T(8,128)}, f32[64,64]{1,0:T(8,128)}, f32[64,64]{1,0:T(8,128)}, f32[64,64]{1,0:T(8,128)}) async-done(((f32[64,64]{1,0:T(8,128)}, f32[64,64]{1,0:T(8,128)}, f32[64,64]{1,0:T(8,128)}, f32[64,64]{1,0:T(8,128)}), (f32[64,64]{1,0:T(8,128)}, f32[64,64]{1,0:T(8,128)}, f32[64,64]{1,0:T(8,128)}, f32[64,64]{1,0:T(8,128)})) %all-reduce.38.cloned.1.call-update) | async-done | bytes 65552 | tf_op jit(solution)/shard_map/psum | solution.py:61
  378.6 14.8 %all-reduce.24.cloned.1.call-done = f32[768,64]{0,1:T(8,128)} async-done(((f32[768,64]{0,1:T(8,128)}), f32[768,64]{0,1:T(8,128)}) %all-reduce.24.cloned.1.call-update) | async-done | bytes 196624 | tf_op jit(solution)/shard_map/psum | solution.py:61
  396.3 8.4 fusion.72
  404.8 8.6 fusion.4
  415.8 27.8 %convolution_bitcast_fusion.4 = f32[4096,64]{0,1:T(8,128)S(1)} fusion(bf16[4096,8192]{1,0:T(8,128)(2,1)} %param.11, f32[8192,64]{0,1:T(8,128)S(1)} %convolution_add_fusion.2), kind=kOutput, calls=%fused_computation.17 | convolution fusion | flops 4295491584 | bytes 70254592 | tf_op jit(solution)/shard_map/dot_general | solution.py:71
  443.6 42.1 %all-reduce.40 = bf16[4096,64]{0,1:T(8,128)(2,1)} all-reduce(f32[4096,64]{0,1:T(8,128)S(1)} %convolution_bitcast_fusion.4), channel_id=1, replica_groups=mesh['samples'=4,'features'=4,'rhs'=2] {'features'}, use_global_device_ids=true, to_apply=%region_12.0 | all-reduce | flops 262144 | bytes 1572864 | tf_op jit(solution)/shard_map/psum | solution.py:72
  485.8 25.9 %convolution_bitcast_fusion.1 = f32[8192,64]{0,1:T(8,128)} fusion(bf16[4096,8192]{1,0:T(8,128)(2,1)} %param.11, bf16[4096,64]{0,1:T(8,128)(2,1)} %all-reduce.40), kind=kOutput, calls=%fused_computation.5 | convolution fusion | flops 4294967296 | bytes 69730304 | tf_op jit(solution)/shard_map/dot_general | solution.py:73
  511.8 20.9 %all-reduce.26.cloned.1.call-done = f32[8192,64]{0,1:T(8,128)} async-done(((f32[8192,64]{0,1:T(8,128)}), f32[8192,64]{0,1:T(8,128)}) %all-reduce.26.cloned.1.call-update) | async-done | bytes 2097168 | tf_op jit(solution)/shard_map/psum | solution.py:14
  537.2 69.3 %all-reduce.28.cloned.1.call-done = f32[8192,64]{0,1:T(8,128)} async-done(((f32[8192,64]{0,1:T(8,128)}), f32[8192,64]{0,1:T(8,128)}) %all-reduce.28.cloned.1.call-update) | async-done | bytes 2097168 | tf_op jit(solution)/shard_map/psum | solution.py:14
  623.6 7.6 fusion.23
  631.4 20.3 %all-reduce.36.cloned.1.call-done = (f32[64,64]{1,0:T(8,128)}, f32[64,64]{1,0:T(8,128)}, f32[64,64]{1,0:T(8,128)}, f32[64,64]{1,0:T(8,128)}) async-done(((f32[64,64]{1,0:T(8,128)}, f32[64,64]{1,0:T(8,128)}, f32[64,64]{1,0:T(8,128)}, f32[64,64]{1,0:T(8,128)}), (f32[64,64]{1,0:T(8,128)}, f32[64,64]{1,0:T(8,128)}, f32[64,64]{1,0:T(8,128)}, f32[64,64]{1,0:T(8,128)})) %all-reduce.36.cloned.1.call-update) | async-done | bytes 65552 | tf_op jit(solution)/shard_map/psum | solution.py:61
  674.8 14.8 %all-reduce.30.cloned.1.call-done = f32[768,64]{0,1:T(8,128)} async-done(((f32[768,64]{0,1:T(8,128)}), f32[768,64]{0,1:T(8,128)}) %all-reduce.30.cloned.1.call-update) | async-done | bytes 196624 | tf_op jit(solution)/shard_map/psum | solution.py:61
  692.6 8.4 fusion.79
  701.1 8.6 fusion.5
  711.9 27.1 %convolution_bitcast_fusion.3 = f32[4096,64]{0,1:T(8,128)S(1)} fusion(bf16[4096,8192]{1,0:T(8,128)(2,1)} %param.11, f32[8192,64]{0,1:T(8,128)S(1)} %convolution_add_fusion), kind=kOutput, calls=%fused_computation.16 | convolution fusion | flops 4295491584 | bytes 70254592 | tf_op jit(solution)/shard_map/dot_general | solution.py:71
  739.0 42.1 %all-reduce.41 = bf16[4096,64]{0,1:T(8,128)(2,1)} all-reduce(f32[4096,64]{0,1:T(8,128)S(1)} %convolution_bitcast_fusion.3), channel_id=1, replica_groups=mesh['samples'=4,'features'=4,'rhs'=2] {'features'}, use_global_device_ids=true, to_apply=%region_20.0 | all-reduce | flops 262144 | bytes 1572864 | tf_op jit(solution)/shard_map/psum | solution.py:72
  781.1 25.9 %convolution_bitcast_fusion = f32[8192,64]{0,1:T(8,128)} fusion(bf16[4096,8192]{1,0:T(8,128)(2,1)} %param.11, bf16[4096,64]{0,1:T(8,128)(2,1)} %all-reduce.41), kind=kOutput, calls=%fused_computation | convolution fusion | flops 4294967296 | bytes 69730304 | tf_op jit(solution)/shard_map/dot_general | solution.py:73
  807.6 20.5 %all-reduce.32.cloned.1.call-done = f32[8192,64]{0,1:T(8,128)} async-done(((f32[8192,64]{0,1:T(8,128)}), f32[8192,64]{0,1:T(8,128)}) %all-reduce.32.cloned.1.call-update) | async-done | bytes 2097168 | tf_op jit(solution)/shard_map/psum | solution.py:14
  838.3 63.6 %all-reduce.34.cloned.1.call-done = f32[8192,64]{0,1:T(8,128)} async-done(((f32[8192,64]{0,1:T(8,128)}), f32[8192,64]{0,1:T(8,128)}) %all-reduce.34.cloned.1.call-update) | async-done | bytes 2097168 | tf_op jit(solution)/shard_map/psum | solution.py:14
  905.4 20.0 %all-reduce = (f32[64,64]{1,0:T(8,128)S(1)}, f32[64,64]{1,0:T(8,128)S(1)}) all-reduce(f32[64,64]{1,0:T(8,128)S(1)} %fusion.19, f32[64,64]{1,0:T(8,128)S(1)} %fusion.83), channel_id=1, replica_groups=mesh['samples'=4,'features'=4,'rhs'=2] {'features'}, use_global_device_ids=true, to_apply=%region_23.28 | all-reduce | flops 8192 | bytes 65536 | tf_op jit(solution)/shard_map/psum | solution.py:61
  (158 shorter events, 144.4 us)
Async XLA Ops:
  7.2 15.7 %all-gather.3.cloned.1.call-start = ((), (), s32[]{:S(2)}) async-start(), calls=%async_computation | async-start | bytes 3145728 | tf_op jit(solution)/shard_map/all_gather | solution.py:56
  7.9 42.4 %all-gather.5.cloned.1.call-start = ((), (), s32[]{:S(2)}) async-start(), calls=%async_computation.1 | async-start | bytes 18874368 | tf_op jit(solution)/shard_map/all_gather | solution.py:58
  8.7 89.1 %all-reduce.18.cloned.1.call-start = ((), (), s32[]{:S(2)}) async-start(), calls=%async_computation.2 | async-start | bytes 393216 | tf_op jit(solution)/shard_map/psum | solution.py:61
  22.8 27.4 %copy-start.1 = (f32[8192,64]{0,1:T(8,128)S(1)}, f32[8192,64]{0,1:T(8,128)}, u32[]{:S(2)}) copy-start(f32[8192,64]{0,1:T(8,128)} %all-gather.3.cloned.1.call-done) | copy-start | bytes 6291460
  50.3 8.2 copy-start
  61.5 175.5 %all-reduce.20.cloned.1.call-start = ((), (), s32[]{:S(2)}) async-start(), calls=%async_computation.3 | async-start | bytes 4194304 | tf_op jit(solution)/shard_map/psum | solution.py:14
  98.7 8.5 copy-start.19
  216.2 94.5 %all-reduce.22.cloned.1.call-start = ((), (), s32[]{:S(2)}) async-start(), calls=%async_computation.4 | async-start | bytes 4194304 | tf_op jit(solution)/shard_map/psum | solution.py:14
  237.0 118.5 %all-reduce.38.cloned.1.call-start = ((), (), s32[]{:S(2)}) async-start(), calls=%async_computation.12 | async-start | bytes 262144 | tf_op jit(solution)/shard_map/psum | solution.py:61
  313.1 2.4 copy-start.4
  315.5 2.4 copy-start.2
  320.4 72.9 %all-reduce.24.cloned.1.call-start = ((), (), s32[]{:S(2)}) async-start(), calls=%async_computation.5 | async-start | bytes 393216 | tf_op jit(solution)/shard_map/psum | solution.py:61
  334.9 197.8 %all-reduce.26.cloned.1.call-start = ((), (), s32[]{:S(2)}) async-start(), calls=%async_computation.6 | async-start | bytes 4194304 | tf_op jit(solution)/shard_map/psum | solution.py:14
  376.3 19.6 %copy-start.24 = (f32[64,64]{1,0:T(8,128)S(1)}, f32[64,64]{1,0:T(8,128)}, u32[]{:S(2)}) copy-start(f32[64,64]{1,0:T(8,128)} %get-tuple-element.14) | copy-start | bytes 49156
  376.3 19.6 %copy-start.25 = (f32[64,64]{1,0:T(8,128)S(1)}, f32[64,64]{1,0:T(8,128)}, u32[]{:S(2)}) copy-start(f32[64,64]{1,0:T(8,128)} %get-tuple-element.15) | copy-start | bytes 49156
  378.4 26.4 %copy-start.7 = (f32[8192,64]{0,1:T(8,128)}, f32[8192,64]{0,1:T(8,128)S(1)}, u32[]{:S(2)}) copy-start(f32[8192,64]{0,1:T(8,128)S(1)} %convolution_subtract_fusion.1) | copy-start | bytes 6291460
  404.8 8.7 copy-start.13
  415.8 117.4 %copy-start.5 = (f32[8192,64]{0,1:T(8,128)}, f32[8192,64]{0,1:T(8,128)S(1)}, u32[]{:S(2)}) copy-start(f32[8192,64]{0,1:T(8,128)S(1)} %convolution_add_fusion.2) | copy-start | bytes 6291460
  511.7 94.8 %all-reduce.28.cloned.1.call-start = ((), (), s32[]{:S(2)}) async-start(), calls=%async_computation.7 | async-start | bytes 4194304 | tf_op jit(solution)/shard_map/psum | solution.py:14
  532.8 119.0 %all-reduce.36.cloned.1.call-start = ((), (), s32[]{:S(2)}) async-start(), calls=%async_computation.11 | async-start | bytes 262144 | tf_op jit(solution)/shard_map/psum | solution.py:61
  606.5 2.9 copy-start.8
  616.7 73.0 %all-reduce.30.cloned.1.call-start = ((), (), s32[]{:S(2)}) async-start(), calls=%async_computation.8 | async-start | bytes 393216 | tf_op jit(solution)/shard_map/psum | solution.py:61
  631.2 196.9 %all-reduce.32.cloned.1.call-start = ((), (), s32[]{:S(2)}) async-start(), calls=%async_computation.9 | async-start | bytes 4194304 | tf_op jit(solution)/shard_map/psum | solution.py:14
  672.5 19.7 %copy-start.22 = (f32[64,64]{1,0:T(8,128)S(1)}, f32[64,64]{1,0:T(8,128)}, u32[]{:S(2)}) copy-start(f32[64,64]{1,0:T(8,128)} %get-tuple-element.10) | copy-start | bytes 49156
  672.5 19.7 %copy-start.23 = (f32[64,64]{1,0:T(8,128)S(1)}, f32[64,64]{1,0:T(8,128)}, u32[]{:S(2)}) copy-start(f32[64,64]{1,0:T(8,128)} %get-tuple-element.11) | copy-start | bytes 49156
  674.6 26.5 %copy-start.10 = (f32[8192,64]{0,1:T(8,128)}, f32[8192,64]{0,1:T(8,128)S(1)}, u32[]{:S(2)}) copy-start(f32[8192,64]{0,1:T(8,128)S(1)} %convolution_subtract_fusion) | copy-start | bytes 6291460
  701.1 8.6 copy-start.14
  807.1 21.1 %copy-start.21 = (f32[64,64]{1,0:T(8,128)S(1)}, f32[64,64]{1,0:T(8,128)}, u32[]{:S(2)}) copy-start(f32[64,64]{1,0:T(8,128)} %copy-done.20) | copy-start | bytes 49156
  807.1 94.8 %all-reduce.34.cloned.1.call-start = ((), (), s32[]{:S(2)}) async-start(), calls=%async_computation.10 | async-start | bytes 4194304 | tf_op jit(solution)/shard_map/psum | solution.py:14
  828.2 5.0 copy-start.15
  833.1 3.3 copy-start.11
  941.9 4.1 copy-start.18
  (10 other events, 19.8 us)
Sparse Core Ops, SparseCore 0:
  9.5 13.2 all-gather.2
  24.4 25.8 all-gather.4
  61.6 36.1 all-reduce.17
  216.3 20.6 all-reduce.19
  240.0 70.6 all-reduce.21
  320.6 34.9 all-reduce.37
  358.4 34.8 all-reduce.23
  511.9 20.8 all-reduce.25
  535.8 70.6 all-reduce.27
  616.8 34.9 all-reduce.35
  654.7 34.9 all-reduce.29
  807.2 20.8 all-reduce.31
  831.2 70.6 all-reduce.33
